TPU v7x, 32 devices: a whole 2x2x4 slice. The times are simulated.
32 devices in a mesh: row: 8 (over z, y), col: 4 (over x, core).
Axes of the slice: x: 2, y: 2, z: 4, core: 2. Of those that a mesh axis runs over, the one named last changes fastest.
Arguments:
- embeddings: bfloat16 [12288, 768], P(('row', 'col'))
- doc_order: int32 [12288], P(('row', 'col')), may hold values from 0 to 12287, each once
Outputs:
- nearest_earlier: float32 [12288], P(('row', 'col'))
Inputs may be any that keep to these rules, and one draw needn't show every extreme that they name: `doc_order`: each value 0 to 12287 appears once.
All inputs are finite; a program needn't handle non-finite values.
Results may differ from a plain program's by a relative error of at most 0.00051.
Values may be sent and summed in bfloat16 or wider, within the bound.
No kernel may reach another device: no remote copies, remote signals or barrier semaphores. Data moves between devices by JAX's collectives and lax.ppermute only.
A program may use at most 64 MiB of HBM per device.

v0:
```python
import jax
import jax.numpy as jnp
from jax import lax
from jax.sharding import PartitionSpec as P


def normalize_rows(embeddings):
    floats = embeddings.astype(jnp.float32)
    scale = lax.rsqrt(jnp.sum(floats * floats, axis=1, keepdims=True) + 1e-06)
    return (floats * scale).astype(jnp.bfloat16)


def block_size(length):
    width = min(512, length)
    while length % width != 0:
        width = width - 1
    return width


def masked_maxima(row_units, row_orders, col_units, col_orders, running):
    length = col_units.shape[0]
    width = block_size(length)
    col_groups = col_units.reshape(length // width, width, col_units.shape[1])
    order_groups = col_orders.reshape(length // width, width)

    def one_block(current, pair):
        units_here, orders_here = pair
        scores = jnp.dot(row_units, units_here.T, preferred_element_type=jnp.float32)
        earlier = orders_here[None, :] < row_orders[:, None]
        masked = jnp.where(earlier, scores, jnp.float32(-1.0))
        return (jnp.maximum(current, jnp.max(masked, axis=1)), None)

    result, unused = lax.scan(one_block, running, (col_groups, order_groups))
    return result


def shards(embeddings, doc_order):
    unit_rows = normalize_rows(embeddings)
    own_rows = unit_rows.shape[0]
    col_count = lax.axis_size("col")
    block_rows = own_rows * col_count
    initial = jnp.full((block_rows,), -1.0, jnp.float32)
    row_units, row_orders = (
        lax.all_gather(unit_rows, "col", axis=0, tiled=True),
        lax.all_gather(doc_order, "col", axis=0, tiled=True),
    )
    best_rows = masked_maxima(
        row_units,
        row_orders,
        lax.all_gather(unit_rows, "row", axis=0, tiled=True),
        lax.all_gather(doc_order, "row", axis=0, tiled=True),
        initial,
    )
    whole_max = lax.pmax(best_rows, "col")
    own_share = lax.dynamic_slice_in_dim(whole_max, lax.axis_index("col") * own_rows, own_rows, 0)
    return jnp.maximum(own_share, jnp.float32(-1.0))


def solution(mesh):
    return jax.shard_map(
        shards,
        mesh=mesh,
        in_specs=(P(("row", "col"), None), P(("row", "col"))),
        out_specs=P(("row", "col")),
        check_vma=False,
    )
```

profile of v0, /device:TPU:0, one launch (start us, length us, event | category | flops | bytes accessed | tf_op | source)
XLA Modules:
  0.0 152.0 jit_solution(297163370144080767)
XLA Ops:
  6.5 0.0 copy-start
  6.5 0.0 all-gather.7.cloned.1.call-start
  6.5 1.3 fusion.5
  7.8 2.0 %fusion.6 = bf16[384,768]{1,0:T(8,128)(2,1)} fusion(bf16[384,768]{1,0:T(8,128)(2,1)} %param.4, f32[384]{0:T(512)S(1)} %add_rsqrt_fusion), kind=kLoop, calls=%fused_computation.11 | loop fusion | flops 884736 | bytes 1181184 | tf_op jit(solution)/shard_map/convert_element_type | solution.py:10
  9.9 0.0 all-gather.7.cloned.1.call-update
  9.9 0.0 all-gather.5.cloned.1.call-start
  9.9 0.7 all-gather.5.cloned.1.call-update
  10.7 0.0 copy-done
  10.7 27.8 %all-gather = s32[8,1,384]{2,1,0:T(1,128)S(1)} all-gather(s32[1,1,384]{2,1,0:T(1,128)S(1)} %reshape.15), channel_id=1, replica_groups=mesh['row'=8,'col'=4] {'row'}, dimensions={0}, use_global_device_ids=true | all-gather | bytes 13824 | tf_op jit(solution)/shard_map/all_gather | solution.py:51
  38.6 5.2 %all-gather.1 = s32[4,1,384]{2,1,0:T(1,128)S(1)} all-gather(s32[1,1,384]{2,1,0:T(1,128)S(1)} %reshape.15), channel_id=1, replica_groups=mesh['row'=8,'col'=4] {'col'}, dimensions={0}, use_global_device_ids=true | all-gather | bytes 7680 | tf_op jit(solution)/shard_map/all_gather | solution.py:45
  43.8 0.0 all-gather.7.cloned.1.call-done
  43.8 74.5 %all-gather.5.cloned.1.call-done = bf16[3072,768]{1,0:T(8,128)(2,1)} async-done(((bf16[384,768]{1,0:T(8,128)(2,1)}), bf16[3072,768]{1,0:T(8,128)(2,1)}) %all-gather.5.cloned.1.call-update) | async-done | bytes 4718608 | tf_op jit(solution)/shard_map/all_gather | solution.py:50
  118.3 20.4 %while.11 = (s32[]{:T(128)}, f32[1536]{0:T(1024)S(1)}, s32[6,512]{1,0:T(8,128)S(1)}, s32[1536]{0:T(1024)S(1)}, bf16[6,512,768]{2,1,0:T(8,128)(2,1)}, /*index=5*/bf16[1536,768]{1,0:T(8,128)(2,1)}, s32[]{:T(128)}, s32[]{:T(128)}) while((s32[]{:T(128)}, f32[1536]{0:T(1024)S(1)}, s32[6,512]{1,0:T(8,128)S(1)}, s32[1536]{0:T(1024)S(1)}, ...), condition=%wide.region_3.4_spmd.clone, body=%wide.region_1.3_spmd.clone.sunk | while | flops 1210320384 | bytes 3183203 | solution.py:33
  118.4 3.3 %fusion.13 = f32[1536]{0:T(1024)S(1)} fusion(bf16[1536,768]{1,0:T(8,128)(2,1)} %get-tuple-element.129, s32[1536]{0:T(1024)S(1)} %get-tuple-element.127, s32[512]{0:T(512)S(1)} %bitcast.20, bf16[6,512,768]{2,1,0:T(8,128)(2,1)} %get-tuple-element.128, s32[]{:T(128)} %get-tuple-element.116), kind=kOutput, calls=%fused_computation.2.clone.1 | convolution fusion | flops 1210317312 | bytes 3160576 | tf_op jit(solution)/shard_map/while/body/eval_jaxpr/dot_general | solution.py:28
  121.8 3.3 %fusion.13 = f32[1536]{0:T(1024)S(1)} fusion(bf16[1536,768]{1,0:T(8,128)(2,1)} %get-tuple-element.129, s32[1536]{0:T(1024)S(1)} %get-tuple-element.127, s32[512]{0:T(512)S(1)} %bitcast.20, bf16[6,512,768]{2,1,0:T(8,128)(2,1)} %get-tuple-element.128, s32[]{:T(128)} %get-tuple-element.116), kind=kOutput, calls=%fused_computation.2.clone.1 | convolution fusion | flops 1210317312 | bytes 3160576 | tf_op jit(solution)/shard_map/while/body/eval_jaxpr/dot_general | solution.py:28
  125.2 3.3 %fusion.13 = f32[1536]{0:T(1024)S(1)} fusion(bf16[1536,768]{1,0:T(8,128)(2,1)} %get-tuple-element.129, s32[1536]{0:T(1024)S(1)} %get-tuple-element.127, s32[512]{0:T(512)S(1)} %bitcast.20, bf16[6,512,768]{2,1,0:T(8,128)(2,1)} %get-tuple-element.128, s32[]{:T(128)} %get-tuple-element.116), kind=kOutput, calls=%fused_computation.2.clone.1 | convolution fusion | flops 1210317312 | bytes 3160576 | tf_op jit(solution)/shard_map/while/body/eval_jaxpr/dot_general | solution.py:28
  128.6 3.3 %fusion.13 = f32[1536]{0:T(1024)S(1)} fusion(bf16[1536,768]{1,0:T(8,128)(2,1)} %get-tuple-element.129, s32[1536]{0:T(1024)S(1)} %get-tuple-element.127, s32[512]{0:T(512)S(1)} %bitcast.20, bf16[6,512,768]{2,1,0:T(8,128)(2,1)} %get-tuple-element.128, s32[]{:T(128)} %get-tuple-element.116), kind=kOutput, calls=%fused_computation.2.clone.1 | convolution fusion | flops 1210317312 | bytes 3160576 | tf_op jit(solution)/shard_map/while/body/eval_jaxpr/dot_general | solution.py:28
  132.0 3.3 %fusion.13 = f32[1536]{0:T(1024)S(1)} fusion(bf16[1536,768]{1,0:T(8,128)(2,1)} %get-tuple-element.129, s32[1536]{0:T(1024)S(1)} %get-tuple-element.127, s32[512]{0:T(512)S(1)} %bitcast.20, bf16[6,512,768]{2,1,0:T(8,128)(2,1)} %get-tuple-element.128, s32[]{:T(128)} %get-tuple-element.116), kind=kOutput, calls=%fused_computation.2.clone.1 | convolution fusion | flops 1210317312 | bytes 3160576 | tf_op jit(solution)/shard_map/while/body/eval_jaxpr/dot_general | solution.py:28
  135.4 3.3 %fusion.13 = f32[1536]{0:T(1024)S(1)} fusion(bf16[1536,768]{1,0:T(8,128)(2,1)} %get-tuple-element.129, s32[1536]{0:T(1024)S(1)} %get-tuple-element.127, s32[512]{0:T(512)S(1)} %bitcast.20, bf16[6,512,768]{2,1,0:T(8,128)(2,1)} %get-tuple-element.128, s32[]{:T(128)} %get-tuple-element.116), kind=kOutput, calls=%fused_computation.2.clone.1 | convolution fusion | flops 1210317312 | bytes 3160576 | tf_op jit(solution)/shard_map/while/body/eval_jaxpr/dot_general | solution.py:28
  138.7 5.8 %pmax.7 = f32[1536]{0:T(1024)S(1)} all-reduce(f32[1536]{0:T(1024)S(1)} %get-tuple-element.37), channel_id=1, replica_groups=mesh['row'=8,'col'=4] {'col'}, use_global_device_ids=true, to_apply=%region_4.5 | all-reduce | flops 1536 | bytes 12288 | tf_op jit(solution)/shard_map/pmax | solution.py:54
  144.5 0.7 dynamic-slice_maximum_fusion
  (19 shorter events, 0.2 us)
Async XLA Ops:
  6.5 4.1 %copy-start = (s32[384]{0:T(512)S(1)}, s32[384]{0:T(512)}, u32[]{:S(2)}) copy-start(s32[384]{0:T(512)} %param.5) | copy-start | bytes 4612
  6.5 37.3 %all-gather.7.cloned.1.call-start = ((), (), s32[]{:S(2)}) async-start(), calls=%async_computation.1 | async-start | bytes 2949120 | tf_op jit(solution)/shard_map/all_gather | solution.py:44
  9.9 108.5 %all-gather.5.cloned.1.call-start = ((), (), s32[]{:S(2)}) async-start(), calls=%async_computation | async-start | bytes 5308416 | tf_op jit(solution)/shard_map/all_gather | solution.py:50
Sparse Core Ops, SparseCore 0:
  10.0 26.7 all-gather.6
  39.0 79.3 all-gather.4
where the time goes:
time: 152 us
  waiting for transfers between devices  75.3 us (50%)
  blocking collectives  38.8 us (26%)
  matrix products  20.1 us (13%)
  between operations  13.5 us (9%)
  other arithmetic  4.08 us (3%)
    all_gather x1, waiting for transfers between devices, shards(): lax.all_gather(unit_rows, 'row', axis=0, tiled=True)  74.5 us
    all_gather x1, blocking collectives, shards(): lax.all_gather(doc_order, 'row', axis=0, tiled=True)  27.8 us
    dot_general x6, matrix products, one_block(): jnp.dot(row_units, units_here.T, preferred_element_type=jnp.float32)  20.1 us
    pmax x1, blocking collectives, shards(): whole_max = lax.pmax(best_rows, 'col')  5.77 us
    all_gather x1, blocking collectives, shards(): lax.all_gather(doc_order, 'col', axis=0, tiled=True)  5.18 us
  transfers between devices with their start and end apart: 2, of which 1 were waited for; matrix products, arithmetic and copies ran while one was open for 0% of the time, Pallas kernels for 0%

commit v1 on v0

--- a/solution.py
+++ b/solution.py
@@ -2,6 +2,18 @@
 import jax.numpy as jnp
 from jax import lax
 from jax.sharding import PartitionSpec as P
+
+
+def doubled_up(array, axis, dim):
+    ways, here = (lax.axis_size(axis), lax.axis_index(axis))
+    grown, reach = (array, 1)
+    while reach < ways:
+        theirs = lax.ppermute(grown, axis, [(d, d ^ reach) for d in range(ways)])
+        mine_first = jnp.concatenate([grown, theirs], axis=dim)
+        theirs_first = jnp.concatenate([theirs, grown], axis=dim)
+        grown = jnp.where(here & reach == 0, mine_first, theirs_first)
+        reach = 2 * reach
+    return grown
 
 
 def normalize_rows(embeddings):
@@ -48,7 +60,7 @@
         row_units,
         row_orders,
         lax.all_gather(unit_rows, "row", axis=0, tiled=True),
-        lax.all_gather(doc_order, "row", axis=0, tiled=True),
+        doubled_up(doc_order, "row", 0),
         initial,
     )
     whole_max = lax.pmax(best_rows, "col")

time: 152 us -> 152 us (level)
  blocking collectives: 38.8 us -> 11.1 us
  waiting for transfers between devices: 75.3 us -> 94.8 us
  starting transfers between devices: 0.04 us -> 8.28 us
    all_gather x1 -> x0, blocking collectives: 27.8 us -> none  [shards(): lax.all_gather(doc_order, 'row', axis=0, tiled=True)]
    all_gather x1, waiting for transfers between devices: 0.02 us -> 9.37 us  [shards(): lax.all_gather(unit_rows, 'col', axis=0, tiled=True)]
    ppermute x0 -> x3, starting transfers between devices: none -> 8.23 us  [doubled_up(): theirs = lax.ppermute(grown, axis, [(d, d ^ reach) for d in range(ways)])]
    all_gather x1, waiting for transfers between devices: 74.5 us -> 81.5 us  [shards(): lax.all_gather(unit_rows, 'row', axis=0, tiled=True)]
    ppermute x0 -> x3, waiting for transfers between devices: none -> 3.15 us  [doubled_up(): theirs = lax.ppermute(grown, axis, [(d, d ^ reach) for d in range(ways)])]
  transfers between devices with their start and end apart: 2 -> 5, of which waited for: 1 -> 4; matrix products, arithmetic and copies ran while one was open for 0% -> 0% of each run, Pallas kernels for 0% -> 0%
where the time goes in v1:
time: 152 us
  waiting for transfers between devices  94.8 us (62%)
  matrix products  20.1 us (13%)
  between operations  13.5 us (9%)
  blocking collectives  11.1 us (7%)
  starting transfers between devices  8.28 us (5%)
  other arithmetic  4.07 us (3%)
    all_gather x1, waiting for transfers between devices, shards(): lax.all_gather(unit_rows, 'row', axis=0, tiled=True)  81.5 us
    dot_general x6, matrix products, one_block(): jnp.dot(row_units, units_here.T, preferred_element_type=jnp.float32)  20.1 us
    all_gather x1, waiting for transfers between devices, shards(): lax.all_gather(unit_rows, 'col', axis=0, tiled=True)  9.37 us
    ppermute x3, starting transfers between devices, doubled_up(): theirs = lax.ppermute(grown, axis, [(d, d ^ reach) for d in range(ways)])  8.23 us
    pmax x1, blocking collectives, shards(): whole_max = lax.pmax(best_rows, 'col')  5.77 us
    all_gather x1, blocking collectives, shards(): lax.all_gather(doc_order, 'col', axis=0, tiled=True)  5.32 us
    ppermute x3, waiting for transfers between devices, doubled_up(): theirs = lax.ppermute(grown, axis, [(d, d ^ reach) for d in range(ways)])  3.15 us
  transfers between devices with their start and end apart: 5, of which 4 were waited for; matrix products, arithmetic and copies ran while one was open for 0% of the time, Pallas kernels for 0%

profile of v1, /device:TPU:0, one launch (start us, length us, event | category | flops | bytes accessed | tf_op | source)
XLA Modules:
  0.0 152.1 jit_solution(14440633916514864618)
XLA Ops:
  6.5 0.0 copy-start
  6.5 0.0 all-gather.6.cloned.1.call-start
  6.5 1.3 fusion.5
  7.8 2.0 %fusion.6 = bf16[384,768]{1,0:T(8,128)(2,1)} fusion(bf16[384,768]{1,0:T(8,128)(2,1)} %param.4, f32[384]{0:T(512)S(1)} %add_rsqrt_fusion), kind=kLoop, calls=%fused_computation.11 | loop fusion | flops 884736 | bytes 1181184 | tf_op jit(solution)/shard_map/convert_element_type | solution.py:22
  9.9 0.0 all-gather.6.cloned.1.call-update
  9.9 0.0 all-gather.4.cloned.1.call-start
  9.9 0.7 all-gather.4.cloned.1.call-update
  10.6 0.0 copy-done
  10.6 3.1 %collective-permute-start = (s32[384]{0:T(512)S(1)}, s32[384]{0:T(512)S(1)}, u32[]{:S(2)}, u32[]{:S(2)}) collective-permute-start(s32[384]{0:T(512)S(1)} %copy-done), channel_id=1, source_target_pairs={{0,4},{4,0},{8,12},{12,8},{16,20},{20,16},{24,28},{28,24},{1,5},{5... | collective-permute-start | bytes 4616 | tf_op jit(solution)/shard_map/ppermute | solution.py:11
  13.7 1.6 %collective-permute-done = s32[384]{0:T(512)S(1)} collective-permute-done((s32[384]{0:T(512)S(1)}, s32[384]{0:T(512)S(1)}, u32[]{:S(2)}, u32[]{:S(2)}) %collective-permute-start) | collective-permute-done | bytes 1568 | tf_op jit(solution)/shard_map/ppermute | solution.py:11
  15.3 2.1 %collective-permute-start.1 = (s32[768]{0:T(1024)S(1)}, s32[768]{0:T(1024)S(1)}, u32[]{:S(2)}, u32[]{:S(2)}) collective-permute-start(s32[768]{0:T(1024)S(1)} %add_select_fusion.2), channel_id=1, source_target_pairs={{0,8},{4,12},{8,0},{12,4},{16,24},{20,28},{24,16},{28,20},{1,9},{5... | collective-permute-start | bytes 9224 | tf_op jit(solution)/shard_map/ppermute | solution.py:11
  17.4 1.6 %collective-permute-done.1 = s32[768]{0:T(1024)S(1)} collective-permute-done((s32[768]{0:T(1024)S(1)}, s32[768]{0:T(1024)S(1)}, u32[]{:S(2)}, u32[]{:S(2)}) %collective-permute-start.1) | collective-permute-done | bytes 3104 | tf_op jit(solution)/shard_map/ppermute | solution.py:11
  18.9 3.1 %collective-permute-start.2 = (s32[1536]{0:T(1024)S(1)}, s32[1536]{0:T(1024)S(1)}, u32[]{:S(2)}, u32[]{:S(2)}) collective-permute-start(s32[1536]{0:T(1024)S(1)} %add_select_fusion.1), channel_id=1, source_target_pairs={{0,16},{4,20},{8,24},{12,28},{16,0},{20,4},{24,8},{28,12},{1,17},{... | collective-permute-start | bytes 18440 | tf_op jit(solution)/shard_map/ppermute | solution.py:11
  22.0 5.3 %all-gather = s32[4,1,384]{2,1,0:T(1,128)S(1)} all-gather(s32[1,1,384]{2,1,0:T(1,128)S(1)} %reshape.20), channel_id=1, replica_groups=mesh['row'=8,'col'=4] {'col'}, dimensions={0}, use_global_device_ids=true | all-gather | bytes 7680 | tf_op jit(solution)/shard_map/all_gather | solution.py:57
  27.4 0.0 collective-permute-done.2
  27.5 9.4 %all-gather.6.cloned.1.call-done = bf16[1536,768]{1,0:T(8,128)(2,1)} async-done(((bf16[384,768]{1,0:T(8,128)(2,1)}), bf16[1536,768]{1,0:T(8,128)(2,1)}) %all-gather.6.cloned.1.call-update) | async-done | bytes 2359312 | tf_op jit(solution)/shard_map/all_gather | solution.py:56
  36.8 81.5 %all-gather.4.cloned.1.call-done = bf16[3072,768]{1,0:T(8,128)(2,1)} async-done(((bf16[384,768]{1,0:T(8,128)(2,1)}), bf16[3072,768]{1,0:T(8,128)(2,1)}) %all-gather.4.cloned.1.call-update) | async-done | bytes 4718608 | tf_op jit(solution)/shard_map/all_gather | solution.py:62
  118.4 20.4 %while.11 = (s32[]{:T(128)}, f32[1536]{0:T(1024)S(1)}, s32[6,512]{1,0:T(8,128)S(1)}, s32[1536]{0:T(1024)S(1)}, bf16[6,512,768]{2,1,0:T(8,128)(2,1)}, /*index=5*/bf16[1536,768]{1,0:T(8,128)(2,1)}, s32[]{:T(128)}, s32[]{:T(128)}) while((s32[]{:T(128)}, f32[1536]{0:T(1024)S(1)}, s32[6,512]{1,0:T(8,128)S(1)}, s32[1536]{0:T(1024)S(1)}, ...), condition=%wide.region_3.4_spmd.clone, body=%wide.region_1.3_spmd.clone.sunk | while | flops 1210320384 | bytes 3183203 | solution.py:45
  118.4 3.3 %fusion.13 = f32[1536]{0:T(1024)S(1)} fusion(bf16[1536,768]{1,0:T(8,128)(2,1)} %get-tuple-element.129, s32[1536]{0:T(1024)S(1)} %get-tuple-element.127, s32[512]{0:T(512)S(1)} %bitcast.20, bf16[6,512,768]{2,1,0:T(8,128)(2,1)} %get-tuple-element.128, s32[]{:T(128)} %get-tuple-element.116), kind=kOutput, calls=%fused_computation.2.clone.1 | convolution fusion | flops 1210317312 | bytes 3160576 | tf_op jit(solution)/shard_map/while/body/eval_jaxpr/dot_general | solution.py:40
  121.8 3.3 %fusion.13 = f32[1536]{0:T(1024)S(1)} fusion(bf16[1536,768]{1,0:T(8,128)(2,1)} %get-tuple-element.129, s32[1536]{0:T(1024)S(1)} %get-tuple-element.127, s32[512]{0:T(512)S(1)} %bitcast.20, bf16[6,512,768]{2,1,0:T(8,128)(2,1)} %get-tuple-element.128, s32[]{:T(128)} %get-tuple-element.116), kind=kOutput, calls=%fused_computation.2.clone.1 | convolution fusion | flops 1210317312 | bytes 3160576 | tf_op jit(solution)/shard_map/while/body/eval_jaxpr/dot_general | solution.py:40
  125.2 3.3 %fusion.13 = f32[1536]{0:T(1024)S(1)} fusion(bf16[1536,768]{1,0:T(8,128)(2,1)} %get-tuple-element.129, s32[1536]{0:T(1024)S(1)} %get-tuple-element.127, s32[512]{0:T(512)S(1)} %bitcast.20, bf16[6,512,768]{2,1,0:T(8,128)(2,1)} %get-tuple-element.128, s32[]{:T(128)} %get-tuple-element.116), kind=kOutput, calls=%fused_computation.2.clone.1 | convolution fusion | flops 1210317312 | bytes 3160576 | tf_op jit(solution)/shard_map/while/body/eval_jaxpr/dot_general | solution.py:40
  128.6 3.3 %fusion.13 = f32[1536]{0:T(1024)S(1)} fusion(bf16[1536,768]{1,0:T(8,128)(2,1)} %get-tuple-element.129, s32[1536]{0:T(1024)S(1)} %get-tuple-element.127, s32[512]{0:T(512)S(1)} %bitcast.20, bf16[6,512,768]{2,1,0:T(8,128)(2,1)} %get-tuple-element.128, s32[]{:T(128)} %get-tuple-element.116), kind=kOutput, calls=%fused_computation.2.clone.1 | convolution fusion | flops 1210317312 | bytes 3160576 | tf_op jit(solution)/shard_map/while/body/eval_jaxpr/dot_general | solution.py:40
  132.0 3.3 %fusion.13 = f32[1536]{0:T(1024)S(1)} fusion(bf16[1536,768]{1,0:T(8,128)(2,1)} %get-tuple-element.129, s32[1536]{0:T(1024)S(1)} %get-tuple-element.127, s32[512]{0:T(512)S(1)} %bitcast.20, bf16[6,512,768]{2,1,0:T(8,128)(2,1)} %get-tuple-element.128, s32[]{:T(128)} %get-tuple-element.116), kind=kOutput, calls=%fused_computation.2.clone.1 | convolution fusion | flops 1210317312 | bytes 3160576 | tf_op jit(solution)/shard_map/while/body/eval_jaxpr/dot_general | solution.py:40
  135.4 3.3 %fusion.13 = f32[1536]{0:T(1024)S(1)} fusion(bf16[1536,768]{1,0:T(8,128)(2,1)} %get-tuple-element.129, s32[1536]{0:T(1024)S(1)} %get-tuple-element.127, s32[512]{0:T(512)S(1)} %bitcast.20, bf16[6,512,768]{2,1,0:T(8,128)(2,1)} %get-tuple-element.128, s32[]{:T(128)} %get-tuple-element.116), kind=kOutput, calls=%fused_computation.2.clone.1 | convolution fusion | flops 1210317312 | bytes 3160576 | tf_op jit(solution)/shard_map/while/body/eval_jaxpr/dot_general | solution.py:40
  138.8 5.8 %pmax.7 = f32[1536]{0:T(1024)S(1)} all-reduce(f32[1536]{0:T(1024)S(1)} %get-tuple-element.37), channel_id=1, replica_groups=mesh['row'=8,'col'=4] {'col'}, use_global_device_ids=true, to_apply=%region_4.5 | all-reduce | flops 1536 | bytes 12288 | tf_op jit(solution)/shard_map/pmax | solution.py:66
  144.6 0.7 dynamic-slice_maximum_fusion
  (22 shorter events, 0.2 us)
Async XLA Ops:
  6.5 4.1 %copy-start = (s32[384]{0:T(512)S(1)}, s32[384]{0:T(512)}, u32[]{:S(2)}) copy-start(s32[384]{0:T(512)} %param.5) | copy-start | bytes 4612
  6.5 30.3 %all-gather.6.cloned.1.call-start = ((), (), s32[]{:S(2)}) async-start(), calls=%async_computation.1 | async-start | bytes 2949120 | tf_op jit(solution)/shard_map/all_gather | solution.py:56
  9.9 108.5 %all-gather.4.cloned.1.call-start = ((), (), s32[]{:S(2)}) async-start(), calls=%async_computation | async-start | bytes 5308416 | tf_op jit(solution)/shard_map/all_gather | solution.py:62
  10.6 4.6 %collective-permute-start = (s32[384]{0:T(512)S(1)}, s32[384]{0:T(512)S(1)}, u32[]{:S(2)}, u32[]{:S(2)}) collective-permute-start(s32[384]{0:T(512)S(1)} %copy-done), channel_id=1, source_target_pairs={{0,4},{4,0},{8,12},{12,8},{16,20},{20,16},{24,28},{28,24},{1,5},{5... | collective-permute-start | bytes 4616 | tf_op jit(solution)/shard_map/ppermute | solution.py:11
  15.3 3.7 %collective-permute-start.1 = (s32[768]{0:T(1024)S(1)}, s32[768]{0:T(1024)S(1)}, u32[]{:S(2)}, u32[]{:S(2)}) collective-permute-start(s32[768]{0:T(1024)S(1)} %add_select_fusion.2), channel_id=1, source_target_pairs={{0,8},{4,12},{8,0},{12,4},{16,24},{20,28},{24,16},{28,20},{1,9},{5... | collective-permute-start | bytes 9224 | tf_op jit(solution)/shard_map/ppermute | solution.py:11
  18.9 8.5 %collective-permute-start.2 = (s32[1536]{0:T(1024)S(1)}, s32[1536]{0:T(1024)S(1)}, u32[]{:S(2)}, u32[]{:S(2)}) collective-permute-start(s32[1536]{0:T(1024)S(1)} %add_select_fusion.1), channel_id=1, source_target_pairs={{0,16},{4,20},{8,24},{12,28},{16,0},{20,4},{24,8},{28,12},{1,17},{... | collective-permute-start | bytes 18440 | tf_op jit(solution)/shard_map/ppermute | solution.py:11
Sparse Core Ops, SparseCore 0:
  10.0 26.7 all-gather.5
  39.0 79.3 all-gather.3
